TPU v7x, 32 devices: a whole 2x2x4 slice. The times are simulated.
32 devices in a mesh: grp: 4 (over z), pair: 8 (over y, x, core).
Axes of the slice: x: 2, y: 2, z: 4, core: 2. Of those that a mesh axis runs over, the one named last changes fastest.
Arguments:
- amplitudes: bfloat16 [64, 512, 512], P('pair', 'grp'), may hold values from -6 to 6
- cholesky: bfloat16 [512, 512, 2048], P('pair', 'grp'), may hold values from -0.09375 to 0.09375
Outputs:
- ladder_term: float32 [512, 4, 64], P('pair', None, 'grp')
All inputs are finite; a program needn't handle non-finite values.
Results may differ from a plain program's by a relative error of at most 0.003.
Values may be sent and summed in bfloat16 or wider, within the bound.
A program may use at most 128 MiB of HBM per device.

v0:
```python
import jax
import jax.numpy as jnp
from jax import lax
from jax.sharding import PartitionSpec as P

A_WIN = 4


def spread(value, axis, source):
    kept = jnp.where(lax.axis_index(axis) == source, value, 0).astype(value.dtype)
    return lax.psum(kept, axis)


def build_tile(chol_local, portion):
    return lax.dot_general(
        chol_local, portion, (((2,), (2,)), ((), ())), preferred_element_type=jnp.float32
    ).astype(jnp.bfloat16)


def ladder(integrals, amp_part):
    return lax.dot_general(
        integrals, amp_part, (((1, 3), (1, 2)), ((), ())), preferred_element_type=jnp.float32
    )


def per_device(amplitudes, cholesky):
    own_window = cholesky[:A_WIN]
    everyone = lax.all_gather(amplitudes, "pair", axis=0, tiled=True)
    shared = spread(own_window, "pair", 0)
    summed = ladder(
        build_tile(cholesky, lax.all_gather(shared, "grp", axis=1, tiled=True)), everyone
    )
    return lax.psum_scatter(summed, "grp", scatter_dimension=2, tiled=True)


def solution(mesh):
    in_specs = (P("pair", "grp", None), P("pair", "grp", None))
    out_specs = P("pair", None, "grp")
    return jax.shard_map(
        per_device, mesh=mesh, in_specs=in_specs, out_specs=out_specs, check_vma=False
    )
```

profile of v0, /device:TPU:0, one launch (start us, length us, event | category | flops | bytes accessed | tf_op | source)
XLA Modules:
  0.0 360.8 jit_solution(16896979740591227450)
XLA Ops:
  6.5 0.0 copy-start
  6.5 0.0 all-reduce.2.cloned.1.call-start
  6.5 3.1 slice_select_fusion
  9.7 0.0 all-reduce.2.cloned.1.call-update
  9.7 0.0 all-gather.3.cloned.1.call-start
  9.7 65.3 %all-reduce.2.cloned.1.call-done = bf16[4,128,2048]{2,1,0:T(8,128)(2,1)} async-done(((bf16[4,128,2048]{2,1,0:T(8,128)(2,1)}), bf16[4,128,2048]{2,1,0:T(8,128)(2,1)}) %all-reduce.2.cloned.1.call-update) | async-done | bytes 2097168 | tf_op jit(solution)/shard_map/psum | solution.py:11
  75.1 0.0 all-gather.3.cloned.1.call-update
  75.1 0.0 all-gather.5.cloned.1.call-start
  75.2 0.0 copy-done
  75.2 1.6 copy.3
  76.7 0.0 all-gather.5.cloned.1.call-update
  76.7 0.0 reduce-scatter.2.cloned.1.call-start
  76.8 148.6 %all-gather.3.cloned.1.call-done = bf16[4,512,2048]{2,1,0:T(8,128)(2,1)} async-done(((bf16[4,128,2048]{2,1,0:T(8,128)(2,1)}), bf16[4,512,2048]{2,1,0:T(8,128)(2,1)}) %all-gather.3.cloned.1.call-update) | async-done | bytes 8388624 | tf_op jit(solution)/shard_map/all_gather | solution.py:31
  225.4 86.3 %fusion.33 = bf16[64,128,4,512]{3,0,1,2:T(8,128)(2,1)} fusion(bf16[64,128,2048,1]{2,1,0,3:T(8,128)(2,1)} %bitcast.34, bf16[4,512,2048]{2,1,0:T(8,128)(2,1)} %all-gather.3.cloned.1.call-done), kind=kOutput, calls=%fused_computation.1.clone.clone.clone.1 | convolution fusion | flops 68736253952 | bytes 75497472 | tf_op jit(solution)/shard_map/dot_general | solution.py:15
  311.7 0.0 all-gather.5.cloned.1.call-done
  311.7 24.7 %fusion.15 = f32[64,4,64]{0,2,1:T(8,128)} fusion(bf16[64,128,512]{2,0,1:T(8,128)(2,1)} %all-gather.5.cloned.1.call-done, bf16[64,128,4,512]{3,0,1,2:T(8,128)(2,1)} %fusion.33), kind=kOutput, calls=%fused_computation.8 | convolution fusion | flops 2147483648 | bytes 42008576 | tf_op jit(solution)/shard_map/dot_general | solution.py:21
  336.5 0.0 reduce-scatter.2.cloned.1.call-update
  336.5 17.8 %reduce-scatter.2.cloned.1.call-done = f32[64,4,16]{0,2,1:T(8,128)} async-done(((f32[64,4,64]{0,2,1:T(8,128)}), f32[64,4,16]{0,2,1:T(8,128)}) %reduce-scatter.2.cloned.1.call-update) | async-done | bytes 16400 | tf_op jit(solution)/shard_map/reduce_scatter | solution.py:33
Async XLA Ops:
  6.5 68.6 %copy-start = (bf16[8,128,512]{2,1,0:T(8,128)(2,1)S(1)}, bf16[8,128,512]{2,1,0:T(8,128)(2,1)}, u32[]{:S(2)}) copy-start(bf16[8,128,512]{2,1,0:T(8,128)(2,1)} %param.2) | copy-start | bytes 3145732
  6.5 68.5 %all-reduce.2.cloned.1.call-start = ((), (), s32[]{:S(2)}) async-start(), calls=%async_computation.1 | async-start | bytes 4194304 | tf_op jit(solution)/shard_map/psum | solution.py:11
  9.7 215.7 %all-gather.3.cloned.1.call-start = ((), (), s32[]{:S(2)}) async-start(), calls=%async_computation.2 | async-start | bytes 10485760 | tf_op jit(solution)/shard_map/all_gather | solution.py:31
  75.1 236.6 %all-gather.5.cloned.1.call-start = ((), (), s32[]{:S(2)}) async-start(), calls=%async_computation.3 | async-start | bytes 9437184 | tf_op jit(solution)/shard_map/all_gather | solution.py:28
  76.7 277.5 %reduce-scatter.2.cloned.1.call-start = ((), (), s32[]{:S(2)}) async-start(), calls=%async_computation.4 | async-start | bytes 163840 | tf_op jit(solution)/shard_map/reduce_scatter | solution.py:33
Sparse Core Ops, SparseCore 0:
  10.6 64.4 all-reduce.1
  76.6 148.6 all-gather.2
  227.3 54.0 all-gather.4
  336.6 17.6 reduce-scatter.1
where the time goes:
time: 361 us
  waiting for transfers between devices  232 us (64%)
  matrix products  111 us (31%)
  between operations  13.1 us (4%)
    all_gather x1, waiting for transfers between devices, per_device(): lax.all_gather(shared, 'grp', axis=1, tiled=True)  149 us
    dot_general x1, matrix products, build_tile(): lax.dot_general(chol_local, portion, (((2,), (2,)), ((), ())), preferred_...  86.3 us
    psum x1, waiting for transfers between devices, spread(): return lax.psum(kept, axis)  65.3 us
    dot_general x1, matrix products, ladder(): lax.dot_general(integrals, amp_part, (((1, 3), (1, 2)), ((), ())), prefer...  24.7 us
    reduce_scatter x1, waiting for transfers between devices, per_device(): return lax.psum_scatter(summed, 'grp', scatter_dimension=2, tiled=True)  17.8 us
  transfers between devices with their start and end apart: 4, of which 3 were waited for; matrix products, arithmetic and copies ran while one was open for 24% of the time, Pallas kernels for 0%

commit v1 on v0

v1 whole, which is shorter than its diff:
```python
import functools
import math

import jax
import jax.numpy as jnp
from jax import lax
from jax.experimental import pallas as pl
from jax.experimental.pallas import tpu as pltpu
from jax.sharding import PartitionSpec as P

A_WIN = 4
CORES = 2
ROWS = 512
LANES = 128


def remote(src, dst, send, recv, where):
    return pltpu.make_async_remote_copy(
        src_ref=src, dst_ref=dst, send_sem=send, recv_sem=recv,
        device_id=where, device_id_type=pl.DeviceIdType.MESH,
    )


def build_kernel(groups, pairs, depth, chol, out, wbuf, lbuf, scr, obuf, lsem, osem, hsem,
                 sc_send, sc_recv, z_send, z_recv, pl_send, pl_recv, cc_send, cc_recv):
    g = lax.axis_index("grp")
    p = lax.axis_index("pair")
    chips = pairs // CORES
    core = lax.rem(p, CORES)
    chip = p // CORES
    mate = p + 1 - 2 * core
    brows, dcount, naux = chol.shape
    piece = dcount // pairs
    blocks = dcount // depth
    total = groups * blocks

    def part(tile, who):
        return wbuf.at[tile, :, pl.ds(pl.multiple_of(who * piece, piece), piece), :]

    def fetch(step, slot):
        at = pl.multiple_of(lax.rem(step, blocks) * depth, depth)
        return pltpu.make_async_copy(chol.at[:, pl.ds(at, depth), :], lbuf.at[slot], lsem.at[slot])

    barrier = pltpu.get_barrier_semaphore()
    for j in range(1, pairs):
        pl.semaphore_signal(barrier, inc=1, device_id={"pair": lax.rem(p + j, pairs)}, device_id_type=pl.DeviceIdType.MESH)
    for j in range(1, groups):
        pl.semaphore_signal(barrier, inc=1, device_id={"grp": lax.rem(g + j, groups)}, device_id_type=pl.DeviceIdType.MESH)
    pl.semaphore_wait(barrier, pairs + groups - 2)

    def scatter(who):
        return remote(chol.at[:A_WIN, who * piece:(who + 1) * piece, :], wbuf.at[g, :, who * piece:(who + 1) * piece, :],
                      sc_send.at[who], sc_recv, {"pair": who})

    @pl.when(p == 0)
    def _():
        for who in list(range(CORES, pairs)) + list(range(1, CORES)):
            scatter(who).start()
        own = pltpu.make_async_copy(chol.at[:A_WIN, :piece, :], wbuf.at[g, :, :piece, :], hsem)
        own.start()
        own.wait()

    @pl.when(p != 0)
    def _():
        remote(part(g, p), part(g, p), sc_send.at[0], sc_recv, {"pair": mate}).wait_recv()

    fetch(0, 0).start()

    def along(j):
        to = lax.rem(g + j, groups)
        return remote(part(g, p), part(g, p), z_send.at[j], z_recv.at[g], {"grp": to})

    def plane(tile, j):
        to = lax.rem(p + CORES * j, pairs)
        return remote(part(tile, p), part(tile, p), pl_send.at[tile, j], pl_recv.at[tile, chip], {"pair": to})

    def plane_in(tile, j):
        source = lax.rem(p + CORES * j, pairs)
        return remote(part(tile, source), part(tile, source), pl_send.at[tile, j],
                      pl_recv.at[tile, source // CORES], {"pair": mate})

    def across(tile, j):
        source = lax.rem(p + CORES * j, pairs)
        return remote(part(tile, source), part(tile, source), cc_send.at[tile, j],
                      cc_recv.at[tile, source // CORES], {"pair": mate})

    def across_in(tile, j):
        source = lax.rem(mate + CORES * j, pairs)
        return remote(part(tile, source), part(tile, source), cc_send.at[tile, j],
                      cc_recv.at[tile, source // CORES], {"pair": mate})

    def spread(tile):
        for j in range(1, chips):
            plane(tile, j).start()
        across(tile, 0).start()

    def forward(tile):
        for j in range(1, chips):
            plane_in(tile, j).wait_recv()
            across(tile, j).start()

    def arrive(tile):
        for j in range(chips):
            across_in(tile, j).wait_recv()

    spread(g)
    for j in range(1, groups):
        along(j).start()
    forward(g)
    arrive(g)

    width = dcount
    group = ROWS // depth

    def put(tile, block, slot):
        at = pl.multiple_of(block * depth, depth)
        return pltpu.make_async_copy(obuf.at[slot], out.at[tile, pl.ds(at, depth)], osem.at[slot])

    for k in range(groups):
        tile = lax.rem(g + k, groups)
        nxt = lax.rem(g + k + 1, groups)
        last = k == groups - 1
        if k > 0:
            arrive(tile)

        def step(block, carry, k=k, tile=tile, nxt=nxt, last=last):
            s = k * blocks + block
            slot = lax.rem(s, 2)
            if not last:
                @pl.when(block == 0)
                def _():
                    remote(part(nxt, p), part(nxt, p), z_send.at[0], z_recv.at[nxt], {"pair": mate}).wait_recv()
                    spread(nxt)

                @pl.when(block == blocks // 2 + 1)
                def _():
                    forward(nxt)

            @pl.when(s + 1 < total)
            def _():
                fetch(s + 1, 1 - slot).start()

            fetch(s, slot).wait()

            @pl.when(s >= 2)
            def _():
                put(tile, block, slot).wait()

            weights = wbuf[tile].reshape(A_WIN * width, naux)
            for part_at in range(brows // group):
                b0 = part_at * group
                rows = lbuf[slot, b0:b0 + group].reshape(group * depth, naux)
                product = lax.dot_general(rows, weights, (((1,), (1,)), ((), ())), preferred_element_type=jnp.float32)
                for n in range(scr.shape[1]):
                    scr[part_at, n] = product[:, n * LANES:(n + 1) * LANES]
                for d in range(depth):
                    for n in range(scr.shape[1]):
                        got = scr[part_at, n, pl.ds(d, group, stride=depth), :].astype(jnp.bfloat16)
                        for off in range(0, LANES, width):
                            obuf[slot, d, (n * LANES + off) // width, b0:b0 + group, :] = got[:, off:off + width]
            put(tile, block, slot).start()
            return carry

        lax.fori_loop(0, blocks, step, 0)

    for s in (total - 2, total - 1):
        put(g, 0, s % 2).wait()

    @pl.when(p == 0)
    def _():
        for who in range(1, pairs):
            scatter(who).wait_send()
    for j in range(1, groups):
        along(j).wait_send()
    for k in range(groups):
        tile = lax.rem(g + k, groups)
        for j in range(chips):
            if j > 0:
                plane(tile, j).wait_send()
            across(tile, j).wait_send()


def build(cholesky, groups, pairs):
    brows, dcount, naux = cholesky.shape
    depth = min(16, dcount)
    chips = pairs // CORES
    width = dcount
    out = jax.ShapeDtypeStruct((groups, dcount, A_WIN, brows, width), jnp.bfloat16)
    dma = pltpu.SemaphoreType.DMA
    return pl.pallas_call(
        functools.partial(build_kernel, groups, pairs, depth),
        out_shape=out,
        in_specs=[pl.BlockSpec(memory_space=pl.ANY)],
        out_specs=pl.BlockSpec(memory_space=pl.ANY),
        scratch_shapes=[
            pltpu.VMEM((groups, A_WIN, width, naux), jnp.bfloat16),
            pltpu.VMEM((2, brows, depth, naux), jnp.bfloat16),
            pltpu.VMEM((brows * depth // ROWS, A_WIN * width // LANES, ROWS, LANES), jnp.float32),
            pltpu.VMEM((2, depth, A_WIN, brows, width), jnp.bfloat16),
            dma((2,)), dma((2,)), dma(()),
            dma((pairs,)), dma(()), dma((groups,)), dma((groups,)),
            dma((groups, chips)), dma((groups, chips)), dma((groups, chips)), dma((groups, chips)),
        ],
        compiler_params=pltpu.CompilerParams(collective_id=0, has_side_effects=True, vmem_limit_bytes=60 * 2**20),
        cost_estimate=pl.CostEstimate(
            flops=2 * brows * dcount * A_WIN * width * groups * naux,
            bytes_accessed=cholesky.size * 2 * groups + math.prod(out.shape) * 2, transcendentals=0),
        name="build",
    )(cholesky)


def ladder_kernel(groups, ints, amps, out, acc, flip, got, send, recv):
    g = lax.axis_index("grp")
    i = pl.program_id(0)
    own = flip.shape[0] // groups
    barrier = pltpu.get_barrier_semaphore()

    def ship(j):
        to = lax.rem(g + j, groups)
        return remote(flip.at[pl.ds(pl.multiple_of(to * own, own), own), :], got.at[j],
                      send.at[j], recv.at[j], {"grp": to})

    @pl.when(i == 0)
    def _():
        for j in range(1, groups):
            pl.semaphore_signal(barrier, inc=1, device_id={"grp": lax.rem(g + j, groups)}, device_id_type=pl.DeviceIdType.MESH)
        pl.semaphore_wait(barrier, groups - 1)
        acc[...] = jnp.zeros_like(acc)

    total = acc[...]
    for d in range(ints.shape[1]):
        left = jnp.concatenate([ints[t, d].reshape(acc.shape[0], ints.shape[4]) for t in range(groups)], axis=1)
        right = amps[:, d].reshape(acc.shape[1], amps.shape[3])
        total = total + lax.dot_general(left, right, (((1,), (1,)), ((), ())), preferred_element_type=jnp.float32)
    acc[...] = total

    @pl.when(i == pl.num_programs(0) - 1)
    def _():
        flip[...] = acc[...].T
        for j in range(1, groups):
            ship(j).start()
        mine = flip[pl.ds(pl.multiple_of(g * own, own), own), :]
        for j in range(1, groups):
            ship(j).wait_recv()
            mine = mine + got[j]
        out[...] = mine
        for j in range(1, groups):
            ship(j).wait_send()


def ladder(ints, amps, groups):
    pairs, dcount, each, virt = amps.shape
    brows, width = ints.shape[3:]
    block = min(8, dcount)
    pair_count = pairs * each
    rows = A_WIN * brows
    return pl.pallas_call(
        functools.partial(ladder_kernel, groups),
        out_shape=jax.ShapeDtypeStruct((pair_count // groups, rows), jnp.float32),
        grid=(dcount // block,),
        in_specs=[
            pl.BlockSpec((groups, block, A_WIN, brows, width), lambda i: (0, i, 0, 0, 0)),
            pl.BlockSpec((pairs, block, each, virt), lambda i: (0, i, 0, 0)),
        ],
        out_specs=pl.BlockSpec((pair_count // groups, rows), lambda i: (0, 0)),
        scratch_shapes=[
            pltpu.VMEM((rows, pair_count), jnp.float32),
            pltpu.VMEM((pair_count, rows), jnp.float32),
            pltpu.VMEM((groups, pair_count // groups, rows), jnp.float32),
            pltpu.SemaphoreType.DMA((groups,)),
            pltpu.SemaphoreType.DMA((groups,)),
        ],
        compiler_params=pltpu.CompilerParams(collective_id=1, has_side_effects=True, vmem_limit_bytes=48 * 2**20),
        cost_estimate=pl.CostEstimate(flops=2 * ints.size * pair_count, bytes_accessed=ints.size * 2 + amps.size * 2, transcendentals=0),
        name="ladder",
    )(ints, amps)


def per_device(groups, pairs, amplitudes, cholesky):
    brows = cholesky.shape[0]
    everyone = lax.all_gather(jnp.transpose(amplitudes, (1, 0, 2)), "pair", axis=0)
    ints = build(cholesky, groups, pairs)
    mine = ladder(ints, everyone, groups)
    return jnp.transpose(mine.reshape(-1, A_WIN, brows), (2, 1, 0))


def solution(mesh):
    in_specs = (P("pair", "grp", None), P("pair", "grp", None))
    return jax.shard_map(
        functools.partial(per_device, mesh.shape["grp"], mesh.shape["pair"]), mesh=mesh,
        in_specs=in_specs, out_specs=P("pair", None, "grp"), check_vma=False,
    )
```

time: 361 us -> 217 us (0.60)
  waiting for transfers between devices: 232 us -> 0.73 us
  Pallas kernels: 0 us -> 188 us
  matrix products: 111 us -> 0 us
  local copies, waits for them, and re-layouts: 1.56 us -> 12 us
    pallas_call x0 -> x2, Pallas kernels: none -> 188 us  [the longest x1 153 us: build(): pl.pallas_call(functools.partial(build_kernel, groups, pairs, depth), out...]
    all_gather x2 -> x1, waiting for transfers between devices: 149 us -> 0.02 us  [per_device(): lax.all_gather(jnp.transpose(amplitudes, (1, 0, 2)), 'pair', axis=0)]
    dot_general x2 -> x0, matrix products: 111 us -> none  [the longest x1 86.3 us: build_tile(): lax.dot_general(chol_local, portion, (((2,), (2,)), ((), ())), preferred_...]
    psum x1 -> x0, waiting for transfers between devices: 65.3 us -> none  [spread(): return lax.psum(kept, axis)]
    reduce_scatter x1 -> x0, waiting for transfers between devices: 17.8 us -> none  [per_device(): return lax.psum_scatter(summed, 'grp', scatter_dimension=2, tiled=True)]
    all_gather x0 -> x1, local copies, waits for them, and re-layouts: none -> 11.3 us  [per_device(): lax.all_gather(jnp.transpose(amplitudes, (1, 0, 2)), 'pair', axis=0)]
  transfers between devices with their start and end apart: 4 -> 1, of which waited for: 3 -> 0; matrix products, arithmetic and copies ran while one was open for 24% -> 0% of each run, Pallas kernels for 0% -> 72%
where the time goes in v1:
time: 217 us; the launch traced here: 214 us
  Pallas kernels  188 us (87%)
  between operations  13.4 us (6%)
  local copies, waits for them, and re-layouts  12 us (6%)
    pallas_call x1, Pallas kernels, build(): pl.pallas_call(functools.partial(build_kernel, groups, pairs, depth), out...  153 us
    pallas_call x1, Pallas kernels, ladder(): pl.pallas_call(functools.partial(ladder_kernel, groups), out_shape=jax.Sh...  34.5 us
    all_gather x1, local copies, waits for them, and re-layouts, per_device(): lax.all_gather(jnp.transpose(amplitudes, (1, 0, 2)), 'pair', axis=0)  11.3 us
  transfers between devices with their start and end apart: 1, of which 0 were waited for; matrix products, arithmetic and copies ran while one was open for 0% of the time, Pallas kernels for 72%

profile of v1, /device:TPU:0, one launch (start us, length us, event | category | flops | bytes accessed | tf_op | source)
XLA Modules:
  0.0 213.9 jit_solution(11631893007651272998)
XLA Ops:
  6.5 0.0 all-gather.3.cloned.1.call-start
  6.5 0.7 all-gather.3.cloned.1.call-update
  7.3 153.3 %build.1.ints = bf16[4,128,4,64,128]{4,3,2,1,0:T(8,128)(2,1)} custom-call(bf16[64,128,2048]{2,1,0:T(8,128)(2,1)} %chol.1), custom_call_target="tpu_custom_call" | custom-call | flops 68719476736 | bytes 167772160 | tf_op jit(solution)/shard_map/build/pallas_call | solution.py:190
  160.5 0.0 all-gather.3.cloned.1.call-done
  160.6 11.3 %copy.3 = bf16[1024,8,512]{2,1,0:T(8,128)(2,1)} copy(bf16[1024,8,512]{2,0,1:T(8,128)(2,1)} %all-gather.3.cloned.1.call-done) | data formatting | bytes 16777216 | tf_op jit(solution)/shard_map/all_gather | solution.py:281
  171.9 34.5 %ladder.1 = f32[16,256]{1,0:T(8,128)S(1)} custom-call(bf16[4,128,4,64,128]{4,3,2,1,0:T(8,128)(2,1)} %build.1.ints, bf16[8,128,8,512]{3,2,1,0:T(8,128)(2,1)} %bitcast.5), custom_call_target="tpu_custom_call" | custom-call | flops 2147483648 | bytes 41943040 | tf_op jit(solution)/shard_map/ladder/pallas_call | solution.py:257
  206.4 0.1 reshape.3
  206.5 0.6 copy.6
Async XLA Ops:
  6.5 154.0 %all-gather.3.cloned.1.call-start = ((), (), s32[]{:S(2)}) async-start(), calls=%async_computation | async-start | bytes 9437184 | tf_op jit(solution)/shard_map/all_gather | solution.py:281
Sparse Core Ops, SparseCore 0:
  9.2 88.0 all-gather.2
